TPU v7x, 256 devices: a whole 4x4x8 slice. The times are simulated.
256 devices in a mesh: row: 16 (over z, core), col: 16 (over x, y).
Axes of the slice: x: 4, y: 4, z: 8, core: 2. Of those that a mesh axis runs over, the one named last changes fastest.
Arguments:
- genotypes: int32 [4096, 16384], P(('row', 'col')), may hold values from 0 to 2, as said below
- snp_index: int32 [4096], P(('row', 'col')), may hold values from 0 to 16383, as said below
- freq_table: float32 [16384], replicated, as said below
- prior: float32 [16384, 16384], P('row', 'col'), as said below
- start_vectors: float32 [16384, 20], P('row'), may hold values from -6 to 6
Outputs:
- grm: float32 [16384, 16384], P('row', 'col')
- pcs: float32 [16384, 20], P('col')
- spectrum: float32 [3, 20], replicated
Inputs may be any that keep to these rules, and one draw needn't show every extreme that they name: `genotypes`: genotype dosages 0, 1 or 2. `snp_index`: strictly increasing; entry j lies in 4 * j to 4 * j + 3. `freq_table`: frequencies are multiples of 1/1024 between 52/1024 and 512/1024. `prior`: exactly symmetric; diagonal between 1 and 2, off-diagonal entries small.
All inputs are finite; a program needn't handle non-finite values.
Results may differ from a plain program's by a relative error of at most 0.0075.
Values may be sent and summed in bfloat16 or wider, within the bound.
No kernel may reach another device: no remote copies, remote signals or barrier semaphores. Data moves between devices by JAX's collectives and lax.ppermute only.
A program may use at most 128 MiB of HBM per device.

v0:
```python
import jax
import jax.numpy as jnp
from jax import lax
from jax.sharding import Mesh
from jax.sharding import PartitionSpec as P

S = 16384
ITERS = 3
COL = ("col_0", "col_1")
ROW_COL = ("row", "col_0", "col_1")


def total_of_pieces(array, axis):
    return lax.all_gather(array, axis).sum(0)


def copy_for_each(array, axis):
    length = lax.axis_size(axis)
    return lax.all_to_all(
        jnp.broadcast_to(array[None], (length, *array.shape)), axis, 0, 0, tiled=True
    )


def taken_together(array, axis):
    return copy_for_each(array, axis).sum(axis=0)


def in_one(arrays, axis):
    ravelled, at, outs = (jnp.concatenate([a.reshape(-1) for a in arrays]), 0, [])
    so_far = taken_together(ravelled, axis)
    for a in arrays:
        outs.append(so_far[at : at + a.size].reshape(a.shape))
        at += a.size
    return tuple(outs)


def one_axis_at_a_time(array, axes):
    for axis in axes:
        array = lax.psum(array, axis)
    return array


def standardize(genotypes, allele_freq):
    doubled = 2.0 * allele_freq
    spread = jnp.sqrt(doubled * (1.0 - allele_freq))
    return (genotypes.astype(jnp.float32) - doubled[:, None]) / spread[:, None]


def orthonormal(factor, image):
    return lax.linalg.triangular_solve(factor, image, left_side=False, lower=True, transpose_a=True)


def apply_tile(tile, vectors, transposed):
    if transposed:
        return lax.dot_general(tile, vectors, (((0,), (0,)), ((), ())))
    return jnp.dot(tile, vectors)


def local_gram(image):
    return jnp.dot(image.T, image)


def body(genotypes, snp_index, freq_table, prior, start_vectors):
    allele_freq = jnp.take(freq_table, snp_index)
    standard = standardize(genotypes, allele_freq).astype(jnp.bfloat16)
    row_count = lax.axis_size("row")
    col_count = lax.axis_size(COL)
    own_snps = genotypes.shape[0]
    total_snps = own_snps * row_count * col_count
    row_piece = lax.all_to_all(standard, "row", split_axis=1, concat_axis=0, tiled=True)
    col_piece = lax.all_to_all(standard, COL, split_axis=1, concat_axis=0, tiled=True)
    col_piece = col_piece.reshape(col_count, 1, own_snps, col_piece.shape[1])
    col_panel = lax.all_gather(col_piece, "row", axis=1, tiled=True)
    col_panel = col_panel.reshape(total_snps, col_panel.shape[3])
    window = lax.dot_general(
        lax.all_gather(row_piece, COL, axis=0, tiled=True),
        col_panel,
        (((0,), (0,)), ((), ())),
        preferred_element_type=jnp.float32,
    )
    grm = prior + window / total_snps
    scaled_start = start_vectors / jnp.sqrt(jnp.float32(S))
    diagonals = []
    image = total_of_pieces(apply_tile(grm, scaled_start, True), "row")
    for step in range(1, ITERS):
        if step % 2 == 1:
            product, gram = in_one((apply_tile(grm, image, False), local_gram(image)), COL)
        else:
            product, gram = (
                total_of_pieces(apply_tile(grm, image, True), "row"),
                total_of_pieces(local_gram(image), "row"),
            )
        factor = jnp.linalg.cholesky(gram)
        diagonals.append(jnp.diagonal(factor))
        image = orthonormal(factor, product)
    gram = one_axis_at_a_time(local_gram(image), COL)
    factor = jnp.linalg.cholesky(gram)
    diagonals.append(jnp.diagonal(factor))
    vectors = orthonormal(factor, image)
    pcs = vectors * jnp.sqrt(jnp.float32(S))
    spectrum = jnp.stack(diagonals, axis=0)
    return (grm, pcs, spectrum)


def solution(mesh):
    finer = Mesh(mesh.devices.reshape(mesh.shape["row"], 4, 4), ("row", "col_0", "col_1"))
    in_specs = (P(ROW_COL, None), P(ROW_COL), P(), P("row", COL), P("row", None))
    out_specs = (P("row", COL), P(COL, None), P())
    return jax.shard_map(body, mesh=finer, in_specs=in_specs, out_specs=out_specs, check_vma=False)
```

profile of v0, /device:TPU:32, one launch (start us, length us, event | category | flops | bytes accessed | tf_op | source)
XLA Modules:
  0.0 351.4 jit_solution(14662210511644327606)
XLA Ops:
  7.2 0.7 compare_select_fusion
  8.0 0.7 gather_fusion
  8.7 0.7 broadcast_multiply_fusion
  9.3 1.4 divide_convert_fusion
  10.8 18.3 %all_to_all.38 = bf16[16,16,1024]{2,0,1:T(8,128)(2,1)S(1)} all-to-all(bf16[16,16,1024]{2,0,1:T(8,128)(2,1)S(1)} %bitcast.82), channel_id=1, replica_groups=mesh['row'=16,'col_0'=4,'col_1'=4] {'col_0','col_1'}, dimensions={1} | all-to-all | bytes 1048576 | tf_op jit(solution)/shard_map/all_to_all | solution.py:71
  29.1 1.1 copy.44
  30.3 25.6 %all_to_all.39 = bf16[16,16,1024]{2,0,1:T(8,128)(2,1)} all-to-all(bf16[16,16,1024]{2,0,1:T(8,128)(2,1)S(1)} %bitcast.83), channel_id=1, replica_groups=mesh['row'=16,'col_0'=4,'col_1'=4] {'row'}, dimensions={1} | all-to-all | bytes 1048576 | tf_op jit(solution)/shard_map/all_to_all | solution.py:70
  55.9 37.5 %all-gather.12.cloned.1.call-done = bf16[16,256,1024]{2,0,1:T(8,128)(2,1)} async-done(((bf16[16,16,1024]{2,0,1:T(8,128)(2,1)}), bf16[16,256,1024]{2,0,1:T(8,128)(2,1)}) %all-gather.12.cloned.1.call-update) | async-done | bytes 8388624 | tf_op jit(solution)/shard_map/all_gather | solution.py:73
  93.5 11.3 %copy.45 = bf16[16,256,1024]{2,1,0:T(8,128)(2,1)} copy(bf16[16,256,1024]{2,0,1:T(8,128)(2,1)} %all-gather.12.cloned.1.call-done) | data formatting | bytes 16777216 | tf_op jit(solution)/shard_map/all_gather | solution.py:73
  104.8 63.9 %all-gather.10.cloned.1.call-done = bf16[4096,1024]{1,0:T(8,128)(2,1)} async-done(((bf16[256,1024]{1,0:T(8,128)(2,1)}), bf16[4096,1024]{1,0:T(8,128)(2,1)}) %all-gather.10.cloned.1.call-update) | async-done | bytes 8388624 | tf_op jit(solution)/shard_map/all_gather | solution.py:76
  168.6 14.4 %multiply_add_fusion = f32[1024,1024]{1,0:T(8,128)S(1)} fusion(f32[1024,1024]{1,0:T(8,128)} %param.11, bf16[4096,1024]{1,0:T(8,128)(2,1)} %all-gather.10.cloned.1.call-done, bf16[4096,1024]{1,0:T(8,128)(2,1)} %bitcast.79), kind=kOutput, calls=%fused_computation.4 | convolution fusion | flops 8592031744 | bytes 25165824 | tf_op jit(solution)/shard_map/dot_general | solution.py:75
  183.0 2.0 copy-done.1
  185.0 1.0 fusion.1
  186.3 38.1 %all-gather.14.cloned.1.call-done = f32[16384,20]{0,1:T(8,128)} async-done(((f32[1024,20]{0,1:T(8,128)}), f32[16384,20]{0,1:T(8,128)}) %all-gather.14.cloned.1.call-update) | async-done | bytes 1310736 | tf_op jit(solution)/shard_map/all_gather | solution.py:14
  224.4 2.5 copy.58
  226.9 0.2 bitcast_reduce_fusion.1
  227.1 0.7 fusion.25
  228.0 0.4 reshape.79
  228.5 0.7 broadcast_in_dim.22
  229.2 27.1 %all_to_all.40 = f32[16,1,20880]{2,1,0:T(1,128)S(1)} all-to-all(f32[16,1,20880]{2,1,0:T(1,128)S(1)} %broadcast_in_dim.22), channel_id=1, replica_groups=mesh['row'=16,'col_0'=4,'col_1'=4] {'col_0','col_1'}, dimensions={0} | all-to-all | bytes 2672640 | tf_op jit(solution)/shard_map/all_to_all | solution.py:19
  256.3 0.8 reduce_sum.37
  257.3 1.8 cholesky.59
  259.2 0.6 compare_reduce_fusion.2
  259.8 0.7 fusion.16
  260.5 1.5 custom-call.13
  262.0 0.6 reshape.82
  262.6 0.6 convolution_bitcast_fusion.2
  263.2 3.2 fusion.27
  266.6 15.7 %all-gather.4 = f32[16,20,20]{2,1,0:T(8,128)S(1)} all-gather(f32[1,20,20]{2,1,0:T(8,128)S(1)} %convolution_bitcast_fusion.3), channel_id=4, replica_groups=mesh['row'=16,'col_0'=4,'col_1'=4] {'row'}, dimensions={0}, use_global_device_ids=true | all-gather | bytes 27200 | tf_op jit(solution)/shard_map/all_gather | solution.py:14
  282.4 1.8 cholesky.70
  284.3 0.6 compare_reduce_fusion.1
  284.9 0.7 fusion.15
  285.6 1.5 custom-call.14
  287.1 0.8 gather_fusion.2
  287.9 0.8 gather_fusion.1
  288.7 12.4 %all-gather.16.cloned.1.call-done = f32[16384,20]{0,1:T(8,128)} async-done(((f32[1024,20]{0,1:T(8,128)}), f32[16384,20]{0,1:T(8,128)}) %all-gather.16.cloned.1.call-update) | async-done | bytes 1310736 | tf_op jit(solution)/shard_map/all_gather | solution.py:14
  301.1 2.3 copy.59
  303.4 0.2 bitcast_reduce_fusion
  303.7 0.3 convolution_bitcast_fusion.1
  304.1 16.8 %psum.14 = f32[20,20]{0,1:T(8,128)S(1)} all-reduce(f32[20,20]{0,1:T(8,128)S(1)} %fusion.28), channel_id=1, replica_groups=mesh['row'=16,'col_0'=4,'col_1'=4] {'col_0'}, use_global_device_ids=true, to_apply=%region_6.9 | all-reduce | flops 400 | bytes 3200 | tf_op jit(solution)/shard_map/psum | solution.py:39
  320.9 16.8 %psum.15 = f32[20,20]{0,1:T(8,128)S(1)} all-reduce(f32[20,20]{0,1:T(8,128)S(1)} %psum.14), channel_id=1, replica_groups=mesh['row'=16,'col_0'=4,'col_1'=4] {'col_1'}, use_global_device_ids=true, to_apply=%region_7.10 | all-reduce | flops 400 | bytes 3200 | tf_op jit(solution)/shard_map/psum | solution.py:39
  337.8 1.8 cholesky.81
  339.7 0.6 compare_reduce_fusion
  340.3 0.7 select_bitcast_fusion
  341.0 0.8 gather_fusion.3
  341.8 1.5 custom-call.15
  343.3 1.0 fusion
  344.2 0.6 pad_maximum_fusion.1
  (37 shorter events, 1.6 us)
Async XLA Ops:
  7.2 0.8 copy-start
  7.2 86.3 %all-gather.12.cloned.1.call-start = ((), (), s32[]{:S(2)}) async-start(), calls=%async_computation.4 | async-start | bytes 8912896 | tf_op jit(solution)/shard_map/all_gather | solution.py:73
  30.2 138.4 %all-gather.10.cloned.1.call-start = ((), (), s32[]{:S(2)}) async-start(), calls=%async_computation.3 | async-start | bytes 8912896 | tf_op jit(solution)/shard_map/all_gather | solution.py:76
  55.9 168.6 %all-gather.14.cloned.1.call-start = ((), (), s32[]{:S(2)}) async-start(), calls=%async_computation.5 | async-start | bytes 1671168 | tf_op jit(solution)/shard_map/all_gather | solution.py:14
  168.6 16.4 %copy-start.3 = (f32[1024,20]{0,1:T(8,128)S(1)}, f32[1024,20]{0,1:T(8,128)}, u32[]{:S(2)}) copy-start(f32[1024,20]{0,1:T(8,128)} %param.12) | copy-start | bytes 245764
  183.0 2.0 copy-start.1
  186.1 115.0 %all-gather.16.cloned.1.call-start = ((), (), s32[]{:S(2)}) async-start(), calls=%async_computation.6 | async-start | bytes 1671168 | tf_op jit(solution)/shard_map/all_gather | solution.py:14
  224.4 2.7 copy-start.2
Sparse Core Ops, SparseCore 0:
  30.4 63.0 all-gather.11
  95.9 72.6 all-gather.9
  186.2 38.1 all-gather.13
  266.6 34.5 all-gather.15
where the time goes:
time: 352 us; the launch traced here: 351 us
  waiting for transfers between devices  152 us (43%)
  blocking collectives  120 us (34%)
  local copies, waits for them, and re-layouts  24.6 us (7%)
  matrix products  21.5 us (6%)
  other arithmetic  18.7 us (5%)
  between operations  13.9 us (4%)
    all_gather x1, waiting for transfers between devices, body(): lax.all_gather(row_piece, COL, axis=0, tiled=True)  63.9 us
    all_gather x2, waiting for transfers between devices, total_of_pieces(): return lax.all_gather(array, axis).sum(0)  50.5 us
    all_gather x1, waiting for transfers between devices, body(): col_panel = lax.all_gather(col_piece, 'row', axis=1, tiled=True)  37.5 us
    psum x2, blocking collectives, one_axis_at_a_time(): array = lax.psum(array, axis)  33.6 us
    all_to_all x1, blocking collectives, copy_for_each(): lax.all_to_all(jnp.broadcast_to(array[None], (length, *array.shape)), axi...  27.1 us
    all_to_all x1, blocking collectives, body(): lax.all_to_all(standard, 'row', split_axis=1, concat_axis=0, tiled=True)  25.6 us
    all_to_all x1, blocking collectives, body(): lax.all_to_all(standard, COL, split_axis=1, concat_axis=0, tiled=True)  18.3 us
    all_gather x1, blocking collectives, total_of_pieces(): return lax.all_gather(array, axis).sum(0)  15.7 us
  transfers between devices with their start and end apart: 4, of which 4 were waited for; matrix products, arithmetic and copies ran while one was open for 5% of the time, Pallas kernels for 0%

commit v1 on v0

--- a/solution.py
+++ b/solution.py
@@ -8,6 +8,27 @@
 ITERS = 3
 COL = ("col_0", "col_1")
 ROW_COL = ("row", "col_0", "col_1")
+
+
+def gather_around(x, axis, dim):
+    size, index, width = (lax.axis_size(axis), lax.axis_index(axis), x.shape[dim])
+    right = [(i, (i + 1) % size) for i in range(size)]
+    left = [(i, (i - 1) % size) for i in range(size)]
+    filled = jnp.zeros((*x.shape[:dim], size * width, *x.shape[dim + 1 :]), x.dtype)
+    filled = lax.dynamic_update_slice_in_dim(filled, x, index * width, axis=dim)
+    from_left = from_right = x
+    halfway = size // 2
+    for step in range(1, halfway + 1):
+        from_left = lax.ppermute(from_left, axis, right)
+        filled = lax.dynamic_update_slice_in_dim(
+            filled, from_left, (index - step) % size * width, axis=dim
+        )
+        if step < size - halfway:
+            from_right = lax.ppermute(from_right, axis, left)
+            filled = lax.dynamic_update_slice_in_dim(
+                filled, from_right, (index + step) % size * width, axis=dim
+            )
+    return filled
 
 
 def total_of_pieces(array, axis):
@@ -70,7 +91,7 @@
     row_piece = lax.all_to_all(standard, "row", split_axis=1, concat_axis=0, tiled=True)
     col_piece = lax.all_to_all(standard, COL, split_axis=1, concat_axis=0, tiled=True)
     col_piece = col_piece.reshape(col_count, 1, own_snps, col_piece.shape[1])
-    col_panel = lax.all_gather(col_piece, "row", axis=1, tiled=True)
+    col_panel = gather_around(col_piece, "row", 1)
     col_panel = col_panel.reshape(total_snps, col_panel.shape[3])
     window = lax.dot_general(
         lax.all_gather(row_piece, COL, axis=0, tiled=True),

time: 352 us -> 317 us (0.901)
  waiting for transfers between devices: 152 us -> 91.5 us
  starting transfers between devices: 0.35 us -> 17.5 us
  local copies, waits for them, and re-layouts: 24.6 us -> 32.7 us
    all_gather x1, waiting for transfers between devices: 63.9 us -> 0.01 us  [body(): lax.all_gather(row_piece, COL, axis=0, tiled=True)]
    ppermute x0 -> x15, waiting for transfers between devices: none -> 39.9 us  [the longest x8 37.4 us: gather_around(): from_left = lax.ppermute(from_left, axis, right)]
    all_gather x1 -> x0, waiting for transfers between devices: 37.5 us -> none  [body(): col_panel = lax.all_gather(col_piece, 'row', axis=1, tiled=True)]
    ppermute x0 -> x15, starting transfers between devices: none -> 17.4 us  [the longest x7 17.4 us: gather_around(): from_right = lax.ppermute(from_right, axis, left)]
    dynamic_update_slice x0 -> x16, local copies, waits for them, and re-layouts: none -> 16.3 us  [the longest x8 8.71 us: gather_around(): lax.dynamic_update_slice_in_dim(filled, from_left, (index - step) % size...]
    all_gather x1 -> x0, local copies, waits for them, and re-layouts: 11.3 us -> none  [body(): col_panel = lax.all_gather(col_piece, 'row', axis=1, tiled=True)]
    broadcast_in_dim x0 -> x1, local copies, waits for them, and re-layouts: none -> 4.28 us  [gather_around(): jnp.zeros((*x.shape[:dim], size * width, *x.shape[dim + 1:]), x.dtype)]
  transfers between devices with their start and end apart: 4 -> 18, of which waited for: 4 -> 12; matrix products, arithmetic and copies ran while one was open for 5% -> 9% of each run, Pallas kernels for 0% -> 0%
where the time goes in v1:
time: 317 us; the launch traced here: 316 us
  blocking collectives  118 us (37%)
  waiting for transfers between devices  91.5 us (29%)
  local copies, waits for them, and re-layouts  32.7 us (10%)
  matrix products  23.7 us (7%)
  other arithmetic  18.7 us (6%)
  starting transfers between devices  17.5 us (6%)
  between operations  13.9 us (4%)
    all_gather x2, waiting for transfers between devices, total_of_pieces(): return lax.all_gather(array, axis).sum(0)  51.5 us
    ppermute x8, waiting for transfers between devices, gather_around(): from_left = lax.ppermute(from_left, axis, right)  37.4 us
    psum x2, blocking collectives, one_axis_at_a_time(): array = lax.psum(array, axis)  33.5 us
    all_to_all x1, blocking collectives, copy_for_each(): lax.all_to_all(jnp.broadcast_to(array[None], (length, *array.shape)), axi...  27.1 us
    all_to_all x1, blocking collectives, body(): lax.all_to_all(standard, 'row', split_axis=1, concat_axis=0, tiled=True)  22.7 us
    all_to_all x1, blocking collectives, body(): lax.all_to_all(standard, COL, split_axis=1, concat_axis=0, tiled=True)  19 us
    ppermute x7, starting transfers between devices, gather_around(): from_right = lax.ppermute(from_right, axis, left)  17.4 us
    all_gather x1, blocking collectives, total_of_pieces(): return lax.all_gather(array, axis).sum(0)  15.7 us
  transfers between devices with their start and end apart: 18, of which 12 were waited for; matrix products, arithmetic and copies ran while one was open for 9% of the time, Pallas kernels for 0%

profile of v1, /device:TPU:32, one launch (start us, length us, event | category | flops | bytes accessed | tf_op | source)
XLA Modules:
  0.0 316.0 jit_solution(5876782824358746015)
XLA Ops:
  9.3 1.4 divide_convert_fusion
  10.8 22.7 %all_to_all.38 = bf16[16,16,1024]{2,0,1:T(8,128)(2,1)} all-to-all(bf16[16,16,1024]{2,0,1:T(8,128)(2,1)S(1)} %bitcast.84), channel_id=1, replica_groups=mesh['row'=16,'col_0'=4,'col_1'=4] {'row'}, dimensions={1} | all-to-all | bytes 1048576 | tf_op jit(solution)/shard_map/all_to_all | solution.py:91
  33.6 19.0 %all_to_all.39 = bf16[16,16,1024]{2,0,1:T(8,128)(2,1)S(1)} all-to-all(bf16[16,16,1024]{2,0,1:T(8,128)(2,1)S(1)} %bitcast.85), channel_id=1, replica_groups=mesh['row'=16,'col_0'=4,'col_1'=4] {'col_0','col_1'}, dimensions={1} | all-to-all | bytes 1048576 | tf_op jit(solution)/shard_map/all_to_all | solution.py:92
  52.5 3.0 collective-permute-start.1
  55.5 6.9 %collective-permute-done = bf16[16,1,16,1024]{3,2,1,0:T(8,128)(2,1)S(1)} collective-permute-done((bf16[16,1,16,1024]{3,2,1,0:T(8,128)(2,1)S(1)}, bf16[16,1,16,1024]{3,2,1,0:T(8,128)(2,1)S(1)}, u32[]{:S(2)}, u32[]{:S(2)}) %collective-permute-start) | collective-permute-done | bytes 524320 | tf_op jit(solution)/shard_map/ppermute | solution.py:22
  62.4 1.7 collective-permute-start.3
  64.2 6.9 %collective-permute-done.2 = bf16[16,1,16,1024]{3,2,1,0:T(8,128)(2,1)S(1)} collective-permute-done((bf16[16,1,16,1024]{3,2,1,0:T(8,128)(2,1)S(1)}, bf16[16,1,16,1024]{3,2,1,0:T(8,128)(2,1)S(1)}, u32[]{:S(2)}, u32[]{:S(2)}) %collective-permute-start.2) | collective-permute-done | bytes 524320 | tf_op jit(solution)/shard_map/ppermute | solution.py:22
  71.0 2.0 collective-permute-start.5
  73.1 6.6 %collective-permute-done.4 = bf16[16,1,16,1024]{3,2,1,0:T(8,128)(2,1)S(1)} collective-permute-done((bf16[16,1,16,1024]{3,2,1,0:T(8,128)(2,1)S(1)}, bf16[16,1,16,1024]{3,2,1,0:T(8,128)(2,1)S(1)}, u32[]{:S(2)}, u32[]{:S(2)}) %collective-permute-start.4) | collective-permute-done | bytes 524320 | tf_op jit(solution)/shard_map/ppermute | solution.py:22
  79.8 2.3 collective-permute-start.7
  82.1 6.3 %collective-permute-done.6 = bf16[16,1,16,1024]{3,2,1,0:T(8,128)(2,1)} collective-permute-done((bf16[16,1,16,1024]{3,2,1,0:T(8,128)(2,1)S(1)}, bf16[16,1,16,1024]{3,2,1,0:T(8,128)(2,1)}, u32[]{:S(2)}, u32[]{:S(2)}) %collective-permute-start.6) | collective-permute-done | bytes 524320 | tf_op jit(solution)/shard_map/ppermute | solution.py:22
  88.8 2.3 collective-permute-start.9
  91.1 6.2 %collective-permute-done.8 = bf16[16,1,16,1024]{3,2,1,0:T(8,128)(2,1)} collective-permute-done((bf16[16,1,16,1024]{3,2,1,0:T(8,128)(2,1)}, bf16[16,1,16,1024]{3,2,1,0:T(8,128)(2,1)}, u32[]{:S(2)}, u32[]{:S(2)}) %collective-permute-start.8) | collective-permute-done | bytes 524320 | tf_op jit(solution)/shard_map/ppermute | solution.py:22
  97.3 4.3 %broadcast_in_dim.25 = bf16[16,16,16,1024]{3,2,1,0:T(8,128)(2,1)} broadcast(bf16[]{:T(256)} %constant.150.clone.1), dimensions={} | broadcast | bytes 8388610 | tf_op jit(solution)/shard_map/broadcast_in_dim | solution.py:17
  102.4 0.8 constant_dynamic-update-slice_fusion.14
  104.8 1.8 collective-permute-start.11
  107.4 0.8 constant_dynamic-update-slice_fusion.10
  108.3 0.8 constant_dynamic-update-slice_fusion.9
  109.1 1.9 constant_dynamic-update-slice_fusion.8
  111.0 1.9 constant_dynamic-update-slice_fusion.7
  113.3 4.2 %collective-permute-start.13 = (bf16[16,1,16,1024]{3,2,1,0:T(8,128)(2,1)S(1)}, bf16[16,1,16,1024]{3,2,1,0:T(8,128)(2,1)S(1)}, u32[]{:S(2)}, u32[]{:S(2)}) collective-permute-start(bf16[16,1,16,1024]{3,2,1,0:T(8,128)(2,1)S(1)} %collective-permute-done.11), channel_id=1, source_target_pairs={{0,240},{16,0},{32,16},{48,32},{64,48},{80,64},{96,80},{112,96},{1... | collective-permute-start | bytes 1572872 | tf_op jit(solution)/shard_map/ppermute | solution.py:27
  117.5 1.9 constant_dynamic-update-slice_fusion.6
  119.4 0.8 constant_dynamic-update-slice_fusion.5
  121.0 0.8 constant_dynamic-update-slice_fusion.3
  121.9 0.8 constant_dynamic-update-slice_fusion.2
  122.7 1.5 collective-permute-done.13
  125.0 4.6 %collective-permute-done.14 = bf16[16,1,16,1024]{3,2,1,0:T(8,128)(2,1)S(1)} collective-permute-done((bf16[16,1,16,1024]{3,2,1,0:T(8,128)(2,1)S(1)}, bf16[16,1,16,1024]{3,2,1,0:T(8,128)(2,1)S(1)}, u32[]{:S(2)}, u32[]{:S(2)}) %collective-permute-start.14) | collective-permute-done | bytes 524320 | tf_op jit(solution)/shard_map/ppermute | solution.py:22
  130.5 14.4 %multiply_add_fusion = f32[1024,1024]{1,0:T(8,128)S(1)} fusion(f32[1024,1024]{1,0:T(8,128)} %param.11, bf16[4096,1024]{1,0:T(8,128)(2,1)} %all-gather.8.cloned.1.call-done, bf16[4096,1024]{1,0:T(8,128)(2,1)} %bitcast.5), kind=kOutput, calls=%fused_computation.4 | convolution fusion | flops 8592031744 | bytes 25165824 | tf_op jit(solution)/shard_map/dot_general | solution.py:96
  144.9 2.0 copy-done.1
  146.9 1.0 fusion.1
  148.0 39.0 %all-gather.10.cloned.1.call-done = f32[16384,20]{0,1:T(8,128)} async-done(((f32[1024,20]{0,1:T(8,128)}), f32[16384,20]{0,1:T(8,128)}) %all-gather.10.cloned.1.call-update) | async-done | bytes 1310736 | tf_op jit(solution)/shard_map/all_gather | solution.py:35
  187.1 2.3 copy.83
  189.6 2.9 fusion.25
  193.9 27.1 %all_to_all.40 = f32[16,1,20880]{2,1,0:T(1,128)S(1)} all-to-all(f32[16,1,20880]{2,1,0:T(1,128)S(1)} %broadcast_in_dim.26), channel_id=1, replica_groups=mesh['row'=16,'col_0'=4,'col_1'=4] {'col_0','col_1'}, dimensions={0} | all-to-all | bytes 2672640 | tf_op jit(solution)/shard_map/all_to_all | solution.py:40
  221.0 0.8 reduce_sum.37
  222.0 1.8 cholesky.59
  225.2 1.5 custom-call.13
  227.9 3.2 %fusion.27 = f32[1024,20]{0,1:T(8,128)} fusion(f32[1024,1024]{1,0:T(8,128)} %copy-done.1, bf16[1024,20]{0,1:T(8,128)(2,1)S(1)} %convolution_bitcast_fusion.2), kind=kOutput, calls=%fused_computation.71 | convolution fusion | flops 41943040 | bytes 4317184 | tf_op jit(solution)/shard_map/dot_general | solution.py:76
  231.3 15.7 %all-gather.3 = f32[16,20,20]{2,1,0:T(8,128)S(1)} all-gather(f32[1,20,20]{2,1,0:T(8,128)S(1)} %convolution_bitcast_fusion.3), channel_id=3, replica_groups=mesh['row'=16,'col_0'=4,'col_1'=4] {'row'}, dimensions={0}, use_global_device_ids=true | all-gather | bytes 27200 | tf_op jit(solution)/shard_map/all_gather | solution.py:35
  247.1 1.8 cholesky.70
  250.3 1.5 custom-call.14
  253.4 12.5 %all-gather.12.cloned.1.call-done = f32[16384,20]{0,1:T(8,128)} async-done(((f32[1024,20]{0,1:T(8,128)}), f32[16384,20]{0,1:T(8,128)}) %all-gather.12.cloned.1.call-update) | async-done | bytes 1310736 | tf_op jit(solution)/shard_map/all_gather | solution.py:35
  265.9 2.3 copy.84
  268.9 16.7 %psum.14 = f32[20,20]{0,1:T(8,128)S(1)} all-reduce(f32[20,20]{0,1:T(8,128)S(1)} %fusion.28), channel_id=1, replica_groups=mesh['row'=16,'col_0'=4,'col_1'=4] {'col_0'}, use_global_device_ids=true, to_apply=%region_6.9 | all-reduce | flops 400 | bytes 3200 | tf_op jit(solution)/shard_map/psum | solution.py:60
  285.6 16.8 %psum.15 = f32[20,20]{0,1:T(8,128)S(1)} all-reduce(f32[20,20]{0,1:T(8,128)S(1)} %psum.14), channel_id=1, replica_groups=mesh['row'=16,'col_0'=4,'col_1'=4] {'col_1'}, use_global_device_ids=true, to_apply=%region_7.10 | all-reduce | flops 400 | bytes 3200 | tf_op jit(solution)/shard_map/psum | solution.py:60
  302.5 1.8 cholesky.81
  306.4 1.5 custom-call.15
  307.9 1.0 fusion
  (81 shorter events, 20.0 us)
Async XLA Ops:
  7.2 0.8 copy-start
  7.2 123.3 %all-gather.8.cloned.1.call-start = ((), (), s32[]{:S(2)}) async-start(), calls=%async_computation.3 | async-start | bytes 8912896 | tf_op jit(solution)/shard_map/all_gather | solution.py:97
  33.5 153.5 %all-gather.10.cloned.1.call-start = ((), (), s32[]{:S(2)}) async-start(), calls=%async_computation.4 | async-start | bytes 1671168 | tf_op jit(solution)/shard_map/all_gather | solution.py:35
  52.5 9.9 %collective-permute-start = (bf16[16,1,16,1024]{3,2,1,0:T(8,128)(2,1)S(1)}, bf16[16,1,16,1024]{3,2,1,0:T(8,128)(2,1)S(1)}, u32[]{:S(2)}, u32[]{:S(2)}) collective-permute-start(bf16[16,1,16,1024]{3,2,1,0:T(8,128)(2,1)S(1)} %bitcast.87), channel_id=1, source_target_pairs={{0,16},{16,32},{32,48},{48,64},{64,80},{80,96},{96,112},{112,128},... | collective-permute-start | bytes 1572872 | tf_op jit(solution)/shard_map/ppermute | solution.py:22
  52.5 9.9 %collective-permute-start.1 = (bf16[16,1,16,1024]{3,2,1,0:T(8,128)(2,1)S(1)}, bf16[16,1,16,1024]{3,2,1,0:T(8,128)(2,1)S(1)}, u32[]{:S(2)}, u32[]{:S(2)}) collective-permute-start(bf16[16,1,16,1024]{3,2,1,0:T(8,128)(2,1)S(1)} %bitcast.88), channel_id=1, source_target_pairs={{0,240},{16,0},{32,16},{48,32},{64,48},{80,64},{96,80},{112,96},{1... | collective-permute-start | bytes 1572872 | tf_op jit(solution)/shard_map/ppermute | solution.py:27
  62.4 8.6 %collective-permute-start.2 = (bf16[16,1,16,1024]{3,2,1,0:T(8,128)(2,1)S(1)}, bf16[16,1,16,1024]{3,2,1,0:T(8,128)(2,1)S(1)}, u32[]{:S(2)}, u32[]{:S(2)}) collective-permute-start(bf16[16,1,16,1024]{3,2,1,0:T(8,128)(2,1)S(1)} %collective-permute-done), channel_id=1, source_target_pairs={{0,16},{16,32},{32,48},{48,64},{64,80},{80,96},{96,112},{112,128},... | collective-permute-start | bytes 1572872 | tf_op jit(solution)/shard_map/ppermute | solution.py:22
  62.4 8.6 %collective-permute-start.3 = (bf16[16,1,16,1024]{3,2,1,0:T(8,128)(2,1)S(1)}, bf16[16,1,16,1024]{3,2,1,0:T(8,128)(2,1)S(1)}, u32[]{:S(2)}, u32[]{:S(2)}) collective-permute-start(bf16[16,1,16,1024]{3,2,1,0:T(8,128)(2,1)S(1)} %collective-permute-done.1), channel_id=1, source_target_pairs={{0,240},{16,0},{32,16},{48,32},{64,48},{80,64},{96,80},{112,96},{1... | collective-permute-start | bytes 1572872 | tf_op jit(solution)/shard_map/ppermute | solution.py:27
  71.0 17.3 %copy-start.2 = (bf16[16,1,16,1024]{3,2,1,0:T(8,128)(2,1)}, bf16[16,1,16,1024]{3,2,1,0:T(8,128)(2,1)S(1)}, u32[]{:S(2)}) copy-start(bf16[16,1,16,1024]{3,2,1,0:T(8,128)(2,1)S(1)} %collective-permute-done.2) | copy-start | bytes 1572868
  71.0 8.6 %collective-permute-start.4 = (bf16[16,1,16,1024]{3,2,1,0:T(8,128)(2,1)S(1)}, bf16[16,1,16,1024]{3,2,1,0:T(8,128)(2,1)S(1)}, u32[]{:S(2)}, u32[]{:S(2)}) collective-permute-start(bf16[16,1,16,1024]{3,2,1,0:T(8,128)(2,1)S(1)} %collective-permute-done.2), channel_id=1, source_target_pairs={{0,16},{16,32},{32,48},{48,64},{64,80},{80,96},{96,112},{112,128},... | collective-permute-start | bytes 1572872 | tf_op jit(solution)/shard_map/ppermute | solution.py:22
  71.0 8.7 %collective-permute-start.5 = (bf16[16,1,16,1024]{3,2,1,0:T(8,128)(2,1)S(1)}, bf16[16,1,16,1024]{3,2,1,0:T(8,128)(2,1)S(1)}, u32[]{:S(2)}, u32[]{:S(2)}) collective-permute-start(bf16[16,1,16,1024]{3,2,1,0:T(8,128)(2,1)S(1)} %collective-permute-done.3), channel_id=1, source_target_pairs={{0,240},{16,0},{32,16},{48,32},{64,48},{80,64},{96,80},{112,96},{1... | collective-permute-start | bytes 1572872 | tf_op jit(solution)/shard_map/ppermute | solution.py:27
  79.6 8.7 %collective-permute-start.6 = (bf16[16,1,16,1024]{3,2,1,0:T(8,128)(2,1)S(1)}, bf16[16,1,16,1024]{3,2,1,0:T(8,128)(2,1)}, u32[]{:S(2)}, u32[]{:S(2)}) collective-permute-start(bf16[16,1,16,1024]{3,2,1,0:T(8,128)(2,1)S(1)} %collective-permute-done.4), channel_id=1, source_target_pairs={{0,16},{16,32},{32,48},{48,64},{64,80},{80,96},{96,112},{112,128},... | collective-permute-start | bytes 1572872 | tf_op jit(solution)/shard_map/ppermute | solution.py:22
  79.8 9.0 %collective-permute-start.7 = (bf16[16,1,16,1024]{3,2,1,0:T(8,128)(2,1)S(1)}, bf16[16,1,16,1024]{3,2,1,0:T(8,128)(2,1)}, u32[]{:S(2)}, u32[]{:S(2)}) collective-permute-start(bf16[16,1,16,1024]{3,2,1,0:T(8,128)(2,1)S(1)} %collective-permute-done.5), channel_id=1, source_target_pairs={{0,240},{16,0},{32,16},{48,32},{64,48},{80,64},{96,80},{112,96},{1... | collective-permute-start | bytes 1572872 | tf_op jit(solution)/shard_map/ppermute | solution.py:27
  88.3 8.9 %collective-permute-start.8 = (bf16[16,1,16,1024]{3,2,1,0:T(8,128)(2,1)}, bf16[16,1,16,1024]{3,2,1,0:T(8,128)(2,1)}, u32[]{:S(2)}, u32[]{:S(2)}) collective-permute-start(bf16[16,1,16,1024]{3,2,1,0:T(8,128)(2,1)} %collective-permute-done.6), channel_id=1, source_target_pairs={{0,16},{16,32},{32,48},{48,64},{64,80},{80,96},{96,112},{112,128},... | collective-permute-start | bytes 1572872 | tf_op jit(solution)/shard_map/ppermute | solution.py:22
  88.3 15.7 %copy-start.3 = (bf16[16,1,16,1024]{3,2,1,0:T(8,128)(2,1)S(1)}, bf16[16,1,16,1024]{3,2,1,0:T(8,128)(2,1)}, u32[]{:S(2)}) copy-start(bf16[16,1,16,1024]{3,2,1,0:T(8,128)(2,1)} %copy-done.2) | copy-start | bytes 1572868
  88.8 16.1 %collective-permute-start.9 = (bf16[16,1,16,1024]{3,2,1,0:T(8,128)(2,1)}, bf16[16,1,16,1024]{3,2,1,0:T(8,128)(2,1)S(1)}, u32[]{:S(2)}, u32[]{:S(2)}) collective-permute-start(bf16[16,1,16,1024]{3,2,1,0:T(8,128)(2,1)} %collective-permute-done.7), channel_id=1, source_target_pairs={{0,240},{16,0},{32,16},{48,32},{64,48},{80,64},{96,80},{112,96},{1... | collective-permute-start | bytes 1572872 | tf_op jit(solution)/shard_map/ppermute | solution.py:27
  97.3 10.2 %collective-permute-start.10 = (bf16[16,1,16,1024]{3,2,1,0:T(8,128)(2,1)}, bf16[16,1,16,1024]{3,2,1,0:T(8,128)(2,1)S(1)}, u32[]{:S(2)}, u32[]{:S(2)}) collective-permute-start(bf16[16,1,16,1024]{3,2,1,0:T(8,128)(2,1)} %collective-permute-done.8), channel_id=1, source_target_pairs={{0,16},{16,32},{32,48},{48,64},{64,80},{80,96},{96,112},{112,128},... | collective-permute-start | bytes 1572872 | tf_op jit(solution)/shard_map/ppermute | solution.py:22
  104.8 8.5 %collective-permute-start.11 = (bf16[16,1,16,1024]{3,2,1,0:T(8,128)(2,1)S(1)}, bf16[16,1,16,1024]{3,2,1,0:T(8,128)(2,1)S(1)}, u32[]{:S(2)}, u32[]{:S(2)}) collective-permute-start(bf16[16,1,16,1024]{3,2,1,0:T(8,128)(2,1)S(1)} %collective-permute-done.9), channel_id=1, source_target_pairs={{0,240},{16,0},{32,16},{48,32},{64,48},{80,64},{96,80},{112,96},{1... | collective-permute-start | bytes 1572872 | tf_op jit(solution)/shard_map/ppermute | solution.py:27
  107.4 12.0 %collective-permute-start.12 = (bf16[16,1,16,1024]{3,2,1,0:T(8,128)(2,1)S(1)}, bf16[16,1,16,1024]{3,2,1,0:T(8,128)(2,1)S(1)}, u32[]{:S(2)}, u32[]{:S(2)}) collective-permute-start(bf16[16,1,16,1024]{3,2,1,0:T(8,128)(2,1)S(1)} %collective-permute-done.10), channel_id=1, source_target_pairs={{0,16},{16,32},{32,48},{48,64},{64,80},{80,96},{96,112},{112,128},... | collective-permute-start | bytes 1572872 | tf_op jit(solution)/shard_map/ppermute | solution.py:22
  113.3 10.9 %collective-permute-start.13 = (bf16[16,1,16,1024]{3,2,1,0:T(8,128)(2,1)S(1)}, bf16[16,1,16,1024]{3,2,1,0:T(8,128)(2,1)S(1)}, u32[]{:S(2)}, u32[]{:S(2)}) collective-permute-start(bf16[16,1,16,1024]{3,2,1,0:T(8,128)(2,1)S(1)} %collective-permute-done.11), channel_id=1, source_target_pairs={{0,240},{16,0},{32,16},{48,32},{64,48},{80,64},{96,80},{112,96},{1... | collective-permute-start | bytes 1572872 | tf_op jit(solution)/shard_map/ppermute | solution.py:27
  119.4 10.3 %collective-permute-start.14 = (bf16[16,1,16,1024]{3,2,1,0:T(8,128)(2,1)S(1)}, bf16[16,1,16,1024]{3,2,1,0:T(8,128)(2,1)S(1)}, u32[]{:S(2)}, u32[]{:S(2)}) collective-permute-start(bf16[16,1,16,1024]{3,2,1,0:T(8,128)(2,1)S(1)} %collective-permute-done.12), channel_id=1, source_target_pairs={{0,16},{16,32},{32,48},{48,64},{64,80},{80,96},{96,112},{112,128},... | collective-permute-start | bytes 1572872 | tf_op jit(solution)/shard_map/ppermute | solution.py:22
  130.5 16.4 %copy-start.4 = (f32[1024,20]{0,1:T(8,128)S(1)}, f32[1024,20]{0,1:T(8,128)}, u32[]{:S(2)}) copy-start(f32[1024,20]{0,1:T(8,128)} %param.12) | copy-start | bytes 245764
  144.9 2.0 copy-start.1
  148.0 117.9 %all-gather.12.cloned.1.call-start = ((), (), s32[]{:S(2)}) async-start(), calls=%async_computation.5 | async-start | bytes 1671168 | tf_op jit(solution)/shard_map/all_gather | solution.py:35
Sparse Core Ops, SparseCore 0:
  33.7 75.8 all-gather.7
  148.1 38.9 all-gather.9
  231.2 34.5 all-gather.11
